TPU v7x, 32 devices: a whole 2x2x4 slice. The times are simulated.
32 devices in a mesh: orb: 4 (over x, core), gx: 2 (over y), gyz: 4 (over z).
Axes of the slice: x: 2, y: 2, z: 4, core: 2. Of those that a mesh axis runs over, the one named last changes fastest.
Arguments:
- orbitals: float32 [2, 12, 32, 32, 128], P(None, 'orb', 'gx', 'gyz'), parts along dimension 1, may hold values from -12 to 12
- potential: float32 [32, 32, 128], P('gx', 'gyz'), may hold values from -8 to 60
Outputs:
- evolved: float32 [2, 12, 32, 32, 128], P(None, 'orb', 'gx', 'gyz'), parts along dimension 1
- residual: float32 [2, 12, 32, 32, 128], P(None, 'orb', 'gx', 'gyz'), parts along dimension 1
There are 4 independent parts, one for each index of `orb`. A program takes and returns all parts, laid end to end along the dimension named above; an argument that names none is the same for every part. Nothing has to cross between parts.
All inputs are finite; a program needn't handle non-finite values.
Results may differ from a plain program's by a relative error of at most 0.0003.
Values sent between devices are 32-bit elements; how exact they have to be, the bound alone decides.
A program may use at most 64 MiB of HBM per device.

v0:
```python
import functools

import jax
import jax.numpy as jnp
from jax import lax
from jax.experimental import pallas as pl
from jax.experimental.pallas import tpu as pltpu
from jax.sharding import PartitionSpec as P

ITERS = 4


SPACING = 0.25
HALF_STEP = 0.05
COEFF_NEAR = 4.0 / 3.0
COEFF_FAR = -1.0 / 12.0
COEFF_SELF = -2.5


def with_halo(array, sides, width):
    for axis, dim in sides:
        size, length = (lax.axis_size(axis), array.shape[dim])
        up = [(i, (i + 1) % size) for i in range(size - 1)]
        down = [(j, i) for i, j in up]
        last = lax.slice_in_dim(array, length - width, length, axis=dim)
        leading = lax.slice_in_dim(array, 0, width, axis=dim)
        before = lax.ppermute(last, axis, up)
        after = lax.ppermute(leading, axis, down)
        array = jnp.concatenate([before, array, after], axis=dim)
    return array


def laplace_apply(padded, potential):
    extent = (padded.shape[2] - 4, padded.shape[3] - 4, padded.shape[4] - 4)

    def window(shift_x, shift_y, shift_z):
        return padded[
            :,
            :,
            2 + shift_x : 2 + shift_x + extent[0],
            2 + shift_y : 2 + shift_y + extent[1],
            2 + shift_z : 2 + shift_z + extent[2],
        ]

    center = window(0, 0, 0)
    summed = 3.0 * COEFF_SELF * center
    for offset, weight in ((1, COEFF_NEAR), (2, COEFF_FAR)):
        summed = summed + weight * (
            window(offset, 0, 0)
            + window(-offset, 0, 0)
            + window(0, offset, 0)
            + window(0, -offset, 0)
            + window(0, 0, offset)
            + window(0, 0, -offset)
        )
    return -0.5 / SPACING**2 * summed + potential * center


def pad_depth(vector):
    return jnp.pad(vector, ((0, 0), (0, 0), (0, 0), (0, 0), (2, 2)))


def system(vector, applied):
    return jnp.stack([vector[0] - HALF_STEP * applied[1], vector[1] + HALF_STEP * applied[0]])


def precondition(vector, potential):
    diagonal = HALF_STEP * (3.75 / SPACING**2 + potential)
    divisor = 1.0 + diagonal * diagonal
    return jnp.stack(
        [(vector[0] + diagonal * vector[1]) / divisor, (vector[1] - diagonal * vector[0]) / divisor]
    )


def braket(left, right):
    real_part = jnp.sum(left[0] * right[0] + left[1] * right[1], axis=(1, 2, 3))
    imag_part = jnp.sum(left[0] * right[1] - left[1] * right[0], axis=(1, 2, 3))
    return (real_part, imag_part)


def times_complex(first, second):
    return (
        first[0] * second[0] - first[1] * second[1],
        first[0] * second[1] + first[1] * second[0],
    )


def divide_complex(first, second):
    modulus = second[0] * second[0] + second[1] * second[1]
    return (
        (first[0] * second[0] + first[1] * second[1]) / modulus,
        (first[1] * second[0] - first[0] * second[1]) / modulus,
    )


def scale_complex(coeff, vector):
    real_coef = coeff[0][:, None, None, None]
    imag_coef = coeff[1][:, None, None, None]
    return jnp.stack(
        [
            real_coef * vector[0] - imag_coef * vector[1],
            real_coef * vector[1] + imag_coef * vector[0],
        ]
    )


def shards(orbitals, potential):

    def apply_shallow(vector):
        padded = with_halo(vector, (("gx", 2), ("gyz", 3)), 2)
        return laplace_apply(pad_depth(padded), potential)

    h_orbitals = apply_shallow(orbitals)
    residual = jnp.stack([2.0 * HALF_STEP * h_orbitals[1], -2.0 * HALF_STEP * h_orbitals[0]])
    evolved = orbitals
    shadow = residual
    direction = residual
    rho_now = lax.psum(braket(shadow, residual), ("gx", "gyz"))
    for iteration in range(ITERS):
        dir_hat = precondition(direction, potential)
        image = system(dir_hat, apply_shallow(dir_hat))
        alpha_step = divide_complex(rho_now, lax.psum(braket(shadow, image), ("gx", "gyz")))
        half_step = residual - scale_complex(alpha_step, image)
        half_hat = precondition(half_step, potential)
        second = system(half_hat, apply_shallow(half_hat))
        cross_local = braket(second, half_step)
        norm_local = jnp.sum(second * second, axis=(0, 2, 3, 4))
        shadow_half = braket(shadow, half_step)
        shadow_second = braket(shadow, second)
        summed = lax.psum(
            (
                cross_local[0],
                cross_local[1],
                norm_local,
                shadow_half[0],
                shadow_half[1],
                shadow_second[0],
                shadow_second[1],
            ),
            ("gx", "gyz"),
        )
        cross_real, cross_imag, norm_second = (summed[0], summed[1], summed[2])
        omega_step = (cross_real / norm_second, cross_imag / norm_second)
        evolved = evolved + scale_complex(alpha_step, dir_hat) + scale_complex(omega_step, half_hat)
        residual = half_step - scale_complex(omega_step, second)
        if iteration + 1 < ITERS:
            along_second = times_complex(omega_step, (summed[5], summed[6]))
            rho_next = (summed[3] - along_second[0], summed[4] - along_second[1])
            beta_step = times_complex(
                divide_complex(rho_next, rho_now), divide_complex(alpha_step, omega_step)
            )
            direction = residual + scale_complex(
                beta_step, direction - scale_complex(omega_step, image)
            )
            rho_now = rho_next
    return (evolved, residual)


UNROLL = 16
LEAD = 8
FIELD_BUDGET = 1 << 20
NEAR = -0.5 / SPACING**2 * COEFF_NEAR * HALF_STEP
FAR = -0.5 / SPACING**2 * COEFF_FAR * HALF_STEP


def owner_of(odd, j, size_x, size_y):
    middle = size_y // 2
    if odd:
        return (1 + j // size_x) % size_x, (middle + j) % size_y
    return j % size_x, (size_y + middle - 1 + j // size_x) % size_y


def sweep(start, stop, plane, carry):
    width = UNROLL if (stop - start) % UNROLL == 0 else 1

    def group(i, carry):
        for k in range(width):
            carry = plane(start + i * width + k, carry)
        return carry

    return lax.fori_loop(0, (stop - start) // width, group, carry)


def solve_kernel(
    sizes,
    orb_hbm,
    pot_hbm,
    evolved_ref,
    residual_ref,
    field,
    hat_a,
    hat_b,
    shadow,
    resid,
    direction,
    image,
    second,
    pot,
    quot,
    quot_d,
    send_orb,
    recv_orb,
    send_pot,
    recv_pot,
    send_out,
    recv_out,
    local_sem,
    orb_ref,
    pot_ref,
):
    size_x, size_y = sizes
    count, bx, by, nz = orb_ref.shape[1:]
    nx, ny = (size_x * bx, size_y * by)
    orb, gx, gy = (lax.axis_index("orb"), lax.axis_index("gx"), lax.axis_index("gyz"))
    me = gx * size_y + gy
    devices = size_x * size_y
    owners = []
    for j in range(count):
        even, odd = (owner_of(parity, j, size_x, size_y) for parity in (0, 1))
        ox = jnp.where(orb % 2 == 1, odd[0], even[0])
        oy = jnp.where(orb % 2 == 1, odd[1], even[1])
        owners.append((ox, oy, jnp.logical_and(ox == gx, oy == gy)))
    mine = owners[0][2]
    for j in range(1, count):
        mine = jnp.logical_or(mine, owners[j][2])

    staged = (
        pltpu.make_async_copy(pot_hbm, pot_ref, local_sem.at[0]),
        pltpu.make_async_copy(orb_hbm, orb_ref, local_sem.at[1]),
    )
    barrier = pltpu.get_barrier_semaphore()
    for dev in range(devices):
        @pl.when(me != dev)
        def _():
            pl.semaphore_signal(
                barrier,
                inc=1,
                device_id={"gx": dev // size_y, "gyz": dev % size_y},
                device_id_type=pl.DeviceIdType.MESH,
            )

    for copy in staged:
        copy.start()

    @pl.when(mine)
    def _():
        for ref in (field, hat_a, hat_b):
            edge = jnp.zeros((2, 2, ny + 2 * LEAD, nz), jnp.float32)
            ref[:, 0:2] = edge
            ref[:, nx + 2 : nx + 4] = edge

            def clear(x, carry):
                side = jnp.zeros((2, LEAD, nz), jnp.float32)
                ref[:, x + 2, 0:LEAD] = side
                ref[:, x + 2, LEAD + ny : 2 * LEAD + ny] = side
                return carry

            lax.fori_loop(0, nx, clear, 0)

    for copy in staged:
        copy.wait()
    pl.semaphore_wait(barrier, devices - 1)

    def spot(ref, x_block, y_block):
        return ref.at[:, pl.ds(2 + x_block * bx, bx), pl.ds(LEAD + y_block * by, by), :]

    def pot_spot(ref, x_block, y_block):
        return ref.at[pl.ds(x_block * bx, bx), pl.ds(y_block * by, by), :]

    def inner_spot(ref, x_block, y_block):
        return ref.at[:, pl.ds(x_block * bx, bx), pl.ds(y_block * by, by), :]

    def remote(src, dst, send, recv, x, y):
        return pltpu.make_async_remote_copy(
            src_ref=src,
            dst_ref=dst,
            send_sem=send,
            recv_sem=recv,
            device_id={"gx": x, "gyz": y},
            device_id_type=pl.DeviceIdType.MESH,
        )

    def gather_copies(j):
        ox, oy, own = owners[j]
        return (
            remote(orb_ref.at[:, j], spot(field, gx, gy), send_orb.at[j], recv_orb.at[me], ox, oy),
            remote(pot_ref, pot_spot(pot, gx, gy), send_pot.at[j], recv_pot.at[me], ox, oy),
        )

    def local_copies(j):
        return (
            pltpu.make_async_copy(orb_ref.at[:, j], spot(field, gx, gy), local_sem.at[0]),
            pltpu.make_async_copy(pot_ref, pot_spot(pot, gx, gy), local_sem.at[1]),
        )

    for j in range(count):
        own = owners[j][2]

        @pl.when(jnp.logical_not(own))
        def _():
            for copy in gather_copies(j):
                copy.start()

        @pl.when(own)
        def _():
            for copy in local_copies(j):
                copy.start()

    lane = lax.broadcasted_iota(jnp.int32, (ny, nz), 1)

    def neighbours(ref, part, x):
        def at(dx, dy):
            return ref[part, x + 2 + dx, LEAD + dy : LEAD + dy + ny, :]

        center = at(0, 0)
        near = (at(1, 0) + at(-1, 0)) + (at(0, 1) + at(0, -1))
        far = (at(2, 0) + at(-2, 0)) + (at(0, 2) + at(0, -2))
        near = near + (
            jnp.where(lane < 1, 0.0, pltpu.roll(center, 1, 1))
            + jnp.where(lane >= nz - 1, 0.0, pltpu.roll(center, nz - 1, 1))
        )
        far = far + (
            jnp.where(lane < 2, 0.0, pltpu.roll(center, 2, 1))
            + jnp.where(lane >= nz - 2, 0.0, pltpu.roll(center, nz - 2, 1))
        )
        return near + (FAR / NEAR) * far, center

    def fold(value):
        return jnp.sum(value.reshape(ny // 8, 8, nz), axis=0)

    def total(value):
        return jnp.sum(value, keepdims=True)

    zero = jnp.zeros((8, nz), jnp.float32)
    rows = slice(LEAD, LEAD + ny)

    def set_hat(hat, x, re, im):
        q, qd = (quot[x], quot_d[x])
        hat[0, x + 2, rows, :] = q * re + qd * im
        hat[1, x + 2, rows, :] = q * im - qd * re

    def start_plane(x, rho):
        d = HALF_STEP * (-1.5 * COEFF_SELF / SPACING**2 + pot[x])
        q = 1.0 / (1.0 + d * d)
        quot[x] = NEAR * q
        quot_d[x] = NEAR * q * d
        off_re, re = neighbours(field, 0, x)
        off_im, im = neighbours(field, 1, x)
        r_re = 2.0 * (NEAR * off_im + d * im)
        r_im = -2.0 * (NEAR * off_re + d * re)
        for ref in (shadow, resid, direction):
            ref[0, x] = r_re
            ref[1, x] = r_im
        set_hat(hat_a, x, r_re, r_im)
        return rho + fold(r_re * r_re + r_im * r_im)

    def image_plane(x, sums):
        off_re, _ = neighbours(hat_a, 0, x)
        off_im, _ = neighbours(hat_a, 1, x)
        i_re = direction[0, x] - off_im
        i_im = direction[1, x] + off_re
        image[0, x] = i_re
        image[1, x] = i_im
        s_re, s_im = (shadow[0, x], shadow[1, x])
        return (
            sums[0] + fold(s_re * i_re + s_im * i_im),
            sums[1] + fold(s_re * i_im - s_im * i_re),
        )

    def half_plane(alpha, x, sums):
        i_re, i_im = (image[0, x], image[1, x])
        h_re = resid[0, x] - (alpha[0] * i_re - alpha[1] * i_im)
        h_im = resid[1, x] - (alpha[0] * i_im + alpha[1] * i_re)
        resid[0, x] = h_re
        resid[1, x] = h_im
        set_hat(hat_b, x, h_re, h_im)
        s_re, s_im = (shadow[0, x], shadow[1, x])
        return (
            sums[0] + fold(s_re * h_re + s_im * h_im),
            sums[1] + fold(s_re * h_im - s_im * h_re),
        )

    def second_plane(x, sums):
        off_re, _ = neighbours(hat_b, 0, x)
        off_im, _ = neighbours(hat_b, 1, x)
        h_re, h_im = (resid[0, x], resid[1, x])
        t_re = h_re - off_im
        t_im = h_im + off_re
        second[0, x] = t_re
        second[1, x] = t_im
        s_re, s_im = (shadow[0, x], shadow[1, x])
        return (
            sums[0] + fold(t_re * h_re + t_im * h_im),
            sums[1] + fold(t_re * h_im - t_im * h_re),
            sums[2] + fold(t_re * t_re + t_im * t_im),
            sums[3] + fold(s_re * t_re + s_im * t_im),
            sums[4] + fold(s_re * t_im - s_im * t_re),
        )

    def update_plane(alpha, omega, x):
        a_re, a_im = (hat_a[0, x + 2, rows, :], hat_a[1, x + 2, rows, :])
        b_re, b_im = (hat_b[0, x + 2, rows, :], hat_b[1, x + 2, rows, :])
        t_re, t_im = (second[0, x], second[1, x])
        step_a, step_b = ((k[0] / NEAR, k[1] / NEAR) for k in (alpha, omega))
        field[0, x + 2, rows, :] = (
            field[0, x + 2, rows, :]
            + (step_a[0] * a_re - step_a[1] * a_im)
            + (step_b[0] * b_re - step_b[1] * b_im)
        )
        field[1, x + 2, rows, :] = (
            field[1, x + 2, rows, :]
            + (step_a[0] * a_im + step_a[1] * a_re)
            + (step_b[0] * b_im + step_b[1] * b_re)
        )
        r_re = resid[0, x] - (omega[0] * t_re - omega[1] * t_im)
        r_im = resid[1, x] - (omega[0] * t_im + omega[1] * t_re)
        resid[0, x] = r_re
        resid[1, x] = r_im
        return r_re, r_im

    def next_plane(alpha, omega, beta, x, carry):
        r_re, r_im = update_plane(alpha, omega, x)
        i_re, i_im = (image[0, x], image[1, x])
        u_re = direction[0, x] - (omega[0] * i_re - omega[1] * i_im)
        u_im = direction[1, x] - (omega[0] * i_im + omega[1] * i_re)
        d_re = r_re + (beta[0] * u_re - beta[1] * u_im)
        d_im = r_im + (beta[0] * u_im + beta[1] * u_re)
        direction[0, x] = d_re
        direction[1, x] = d_im
        set_hat(hat_a, x, d_re, d_im)
        return carry

    def out_copies(j, x, y):
        slot = x * size_y + y
        return (
            remote(
                spot(field, x, y), evolved_ref.at[:, j], send_out.at[0, slot], recv_out.at[0, j], x, y
            ),
            remote(
                inner_spot(resid, x, y),
                residual_ref.at[:, j],
                send_out.at[1, slot],
                recv_out.at[1, j],
                x,
                y,
            ),
        )

    def out_local(j):
        return (
            pltpu.make_async_copy(spot(field, gx, gy), evolved_ref.at[:, j], local_sem.at[0]),
            pltpu.make_async_copy(inner_spot(resid, gx, gy), residual_ref.at[:, j], local_sem.at[1]),
        )

    def each_out(x, act):
        for j in range(count):
            for y in range(size_y):
                other = jnp.logical_or(gx != x, gy != y)

                @pl.when(jnp.logical_and(owners[j][2], other))
                def _():
                    for copy in out_copies(j, x, y):
                        act(copy)

                @pl.when(jnp.logical_and(owners[j][2], jnp.logical_not(other)))
                def _():
                    for copy in out_local(j):
                        if act is begin:
                            copy.start()
                        else:
                            copy.wait()

    def begin(copy):
        copy.start()

    def finish(copy):
        copy.wait_send()

    @pl.when(mine)
    def _():
        for dev in range(devices):
            x, y = (dev // size_y, dev % size_y)

            @pl.when(me != dev)
            def _():
                remote(
                    orb_ref.at[:, 0], spot(field, x, y), send_orb.at[0], recv_orb.at[dev], x, y
                ).wait_recv()
                remote(
                    pot_ref, pot_spot(pot, x, y), send_pot.at[0], recv_pot.at[dev], x, y
                ).wait_recv()

        for copy in local_copies(0):
            copy.wait()

        rho_sum = sweep(0, nx, start_plane, zero)
        rho = (total(rho_sum), jnp.zeros((1, 1), jnp.float32))
        for iteration in range(ITERS):
            sums = sweep(0, nx, image_plane, (zero, zero))
            alpha = divide_complex(rho, (total(sums[0]), total(sums[1])))
            held = sweep(0, nx, functools.partial(half_plane, alpha), (zero, zero))
            sums = sweep(0, nx, second_plane, (zero,) * 5)
            norm = total(sums[2])
            omega = (total(sums[0]) / norm, total(sums[1]) / norm)
            if iteration + 1 < ITERS:
                along = times_complex(omega, (total(sums[3]), total(sums[4])))
                rho_next = (total(held[0]) - along[0], total(held[1]) - along[1])
                beta = times_complex(divide_complex(rho_next, rho), divide_complex(alpha, omega))
                rho = rho_next
                sweep(0, nx, functools.partial(next_plane, alpha, omega, beta), 0)

        def last_plane(x, carry):
            update_plane(alpha, omega, x)
            return carry

        for x in range(size_x):
            sweep(x * bx, (x + 1) * bx, last_plane, 0)
            each_out(x, begin)
        for x in range(size_x):
            each_out(x, finish)

    for j in range(count):
        @pl.when(jnp.logical_not(owners[j][2]))
        def _():
            for copy in gather_copies(j):
                copy.wait_send()
            for copy in out_copies(j, 0, 0):
                copy.wait_recv()


def gathered(sizes, orbitals, potential):
    size_x, size_y = sizes
    _, count, bx, by, nz = orbitals.shape
    nx, ny = (size_x * bx, size_y * by)
    padded = pltpu.VMEM((2, nx + 4, ny + 2 * LEAD, nz), jnp.float32)
    plain = pltpu.VMEM((2, nx, ny, nz), jnp.float32)
    scalar = pltpu.VMEM((nx, ny, nz), jnp.float32)
    dma = pltpu.SemaphoreType.DMA
    devices = size_x * size_y
    shape = jax.ShapeDtypeStruct(orbitals.shape, jnp.float32)
    return pl.pallas_call(
        functools.partial(solve_kernel, sizes),
        out_shape=(shape, shape),
        in_specs=[pl.BlockSpec(memory_space=pltpu.HBM)] * 2,
        out_specs=(pl.BlockSpec(memory_space=pltpu.VMEM),) * 2,
        scratch_shapes=[padded] * 3
        + [plain] * 5
        + [scalar] * 3
        + [
            dma((count,)),
            dma((devices,)),
            dma((count,)),
            dma((devices,)),
            dma((2, devices)),
            dma((2, count)),
            dma((2,)),
            pltpu.VMEM(orbitals.shape, jnp.float32),
            pltpu.VMEM(potential.shape, jnp.float32),
        ],
        compiler_params=pltpu.CompilerParams(
            collective_id=0, has_side_effects=True, vmem_limit_bytes=48 * 1024 * 1024
        ),
    )(orbitals, potential)


def step(sizes, orbitals, potential):
    _, count, bx, by, nz = orbitals.shape
    devices = sizes[0] * sizes[1]
    fits = 8 * devices * bx * by * nz <= FIELD_BUDGET
    distinct = all(
        len({owner_of(parity, j, *sizes) for j in range(count)}) == count for parity in (0, 1)
    )
    if fits and distinct and by % 8 == 0 and nz % 128 == 0:
        return gathered(sizes, orbitals, potential)
    return shards(orbitals, potential)


def solution(mesh):
    sizes = (mesh.shape["gx"], mesh.shape["gyz"])
    return jax.shard_map(
        functools.partial(step, sizes),
        mesh=mesh,
        in_specs=(P(None, "orb", "gx", "gyz", None), P("gx", "gyz", None)),
        out_specs=(P(None, "orb", "gx", "gyz", None), P(None, "orb", "gx", "gyz", None)),
        check_vma=False,
    )
```

profile of v0, /device:TPU:28, one launch (start us, length us, event | category | flops | bytes accessed | tf_op | source)
XLA Modules:
  0.0 60.3 jit_solution(1541422738158516135)
XLA Ops:
  0.6 0.0 copy-start
  0.6 1.0 %copy-done = f32[2,3,16,8,128]{4,3,2,1,0:T(8,128)S(1)} copy-done((f32[2,3,16,8,128]{4,3,2,1,0:T(8,128)S(1)}, f32[2,3,16,8,128]{4,3,2,1,0:T(8,128)}, u32[]{:S(2)}) %copy-start) | copy-done | bytes 393240
  1.6 0.0 copy-start.1
  1.6 0.8 %copy-done.1 = f32[16,8,128]{2,1,0:T(8,128)S(1)} copy-done((f32[16,8,128]{2,1,0:T(8,128)S(1)}, f32[16,8,128]{2,1,0:T(8,128)}, u32[]{:S(2)}) %copy-start.1) | copy-done | bytes 65560
  2.5 56.3 %shard_map.41 = (f32[2,3,16,8,128]{4,3,2,1,0:T(8,128)S(1)}, f32[2,3,16,8,128]{4,3,2,1,0:T(8,128)S(1)}) custom-call(f32[2,3,16,8,128]{4,3,2,1,0:T(8,128)S(1)} %copy-done, f32[16,8,128]{2,1,0:T(8,128)S(1)} %copy-done.1), custom_call_target="tpu_custom_call" | custom-call | tf_op jit(solution)/shard_map/pallas_call | solution.py:541
  58.8 0.7 %copy.6 = f32[2,3,16,8,128]{4,3,2,1,0:T(8,128)} copy(f32[2,3,16,8,128]{4,3,2,1,0:T(8,128)S(1)} %get-tuple-element.4) | data formatting | bytes 786432
  59.6 0.7 %copy.7 = f32[2,3,16,8,128]{4,3,2,1,0:T(8,128)} copy(f32[2,3,16,8,128]{4,3,2,1,0:T(8,128)S(1)} %get-tuple-element.5) | data formatting | bytes 786432
Async XLA Ops:
  0.6 1.0 %copy-start = (f32[2,3,16,8,128]{4,3,2,1,0:T(8,128)S(1)}, f32[2,3,16,8,128]{4,3,2,1,0:T(8,128)}, u32[]{:S(2)}) copy-start(f32[2,3,16,8,128]{4,3,2,1,0:T(8,128)} %orb_hbm.1) | copy-start | bytes 1179652
  1.6 0.8 %copy-start.1 = (f32[16,8,128]{2,1,0:T(8,128)S(1)}, f32[16,8,128]{2,1,0:T(8,128)}, u32[]{:S(2)}) copy-start(f32[16,8,128]{2,1,0:T(8,128)} %pot_hbm.1) | copy-start | bytes 196612
where the time goes:
time: 60.5 us; the launch traced here: 60.3 us
  Pallas kernels  56.3 us (93%)
  local copies, waits for them, and re-layouts  3.32 us (5%)
  between operations  0.65 us (1%)
    pallas_call x1, Pallas kernels, gathered(): pl.pallas_call(functools.partial(solve_kernel, sizes), out_shape=(shape,...  56.3 us
    unnamed x6, local copies, waits for them, and re-layouts  3.32 us

commit v1 on v0

v1 whole, which is shorter than its diff:
```python
import functools

import jax
import jax.numpy as jnp
from jax import lax
from jax.experimental import pallas as pl
from jax.experimental.pallas import tpu as pltpu
from jax.sharding import PartitionSpec as P

ITERS = 4


SPACING = 0.25
HALF_STEP = 0.05
COEFF_NEAR = 4.0 / 3.0
COEFF_FAR = -1.0 / 12.0
COEFF_SELF = -2.5


def with_halo(array, sides, width):
    for axis, dim in sides:
        size, length = (lax.axis_size(axis), array.shape[dim])
        up = [(i, (i + 1) % size) for i in range(size - 1)]
        down = [(j, i) for i, j in up]
        last = lax.slice_in_dim(array, length - width, length, axis=dim)
        leading = lax.slice_in_dim(array, 0, width, axis=dim)
        before = lax.ppermute(last, axis, up)
        after = lax.ppermute(leading, axis, down)
        array = jnp.concatenate([before, array, after], axis=dim)
    return array


def laplace_apply(padded, potential):
    extent = (padded.shape[2] - 4, padded.shape[3] - 4, padded.shape[4] - 4)

    def window(shift_x, shift_y, shift_z):
        return padded[
            :,
            :,
            2 + shift_x : 2 + shift_x + extent[0],
            2 + shift_y : 2 + shift_y + extent[1],
            2 + shift_z : 2 + shift_z + extent[2],
        ]

    center = window(0, 0, 0)
    summed = 3.0 * COEFF_SELF * center
    for offset, weight in ((1, COEFF_NEAR), (2, COEFF_FAR)):
        summed = summed + weight * (
            window(offset, 0, 0)
            + window(-offset, 0, 0)
            + window(0, offset, 0)
            + window(0, -offset, 0)
            + window(0, 0, offset)
            + window(0, 0, -offset)
        )
    return -0.5 / SPACING**2 * summed + potential * center


def pad_depth(vector):
    return jnp.pad(vector, ((0, 0), (0, 0), (0, 0), (0, 0), (2, 2)))


def system(vector, applied):
    return jnp.stack([vector[0] - HALF_STEP * applied[1], vector[1] + HALF_STEP * applied[0]])


def precondition(vector, potential):
    diagonal = HALF_STEP * (3.75 / SPACING**2 + potential)
    divisor = 1.0 + diagonal * diagonal
    return jnp.stack(
        [(vector[0] + diagonal * vector[1]) / divisor, (vector[1] - diagonal * vector[0]) / divisor]
    )


def braket(left, right):
    real_part = jnp.sum(left[0] * right[0] + left[1] * right[1], axis=(1, 2, 3))
    imag_part = jnp.sum(left[0] * right[1] - left[1] * right[0], axis=(1, 2, 3))
    return (real_part, imag_part)


def times_complex(first, second):
    return (
        first[0] * second[0] - first[1] * second[1],
        first[0] * second[1] + first[1] * second[0],
    )


def divide_complex(first, second):
    modulus = second[0] * second[0] + second[1] * second[1]
    return (
        (first[0] * second[0] + first[1] * second[1]) / modulus,
        (first[1] * second[0] - first[0] * second[1]) / modulus,
    )


def scale_complex(coeff, vector):
    real_coef = coeff[0][:, None, None, None]
    imag_coef = coeff[1][:, None, None, None]
    return jnp.stack(
        [
            real_coef * vector[0] - imag_coef * vector[1],
            real_coef * vector[1] + imag_coef * vector[0],
        ]
    )


def shards(orbitals, potential):

    def apply_shallow(vector):
        padded = with_halo(vector, (("gx", 2), ("gyz", 3)), 2)
        return laplace_apply(pad_depth(padded), potential)

    h_orbitals = apply_shallow(orbitals)
    residual = jnp.stack([2.0 * HALF_STEP * h_orbitals[1], -2.0 * HALF_STEP * h_orbitals[0]])
    evolved = orbitals
    shadow = residual
    direction = residual
    rho_now = lax.psum(braket(shadow, residual), ("gx", "gyz"))
    for iteration in range(ITERS):
        dir_hat = precondition(direction, potential)
        image = system(dir_hat, apply_shallow(dir_hat))
        alpha_step = divide_complex(rho_now, lax.psum(braket(shadow, image), ("gx", "gyz")))
        half_step = residual - scale_complex(alpha_step, image)
        half_hat = precondition(half_step, potential)
        second = system(half_hat, apply_shallow(half_hat))
        cross_local = braket(second, half_step)
        norm_local = jnp.sum(second * second, axis=(0, 2, 3, 4))
        shadow_half = braket(shadow, half_step)
        shadow_second = braket(shadow, second)
        summed = lax.psum(
            (
                cross_local[0],
                cross_local[1],
                norm_local,
                shadow_half[0],
                shadow_half[1],
                shadow_second[0],
                shadow_second[1],
            ),
            ("gx", "gyz"),
        )
        cross_real, cross_imag, norm_second = (summed[0], summed[1], summed[2])
        omega_step = (cross_real / norm_second, cross_imag / norm_second)
        evolved = evolved + scale_complex(alpha_step, dir_hat) + scale_complex(omega_step, half_hat)
        residual = half_step - scale_complex(omega_step, second)
        if iteration + 1 < ITERS:
            along_second = times_complex(omega_step, (summed[5], summed[6]))
            rho_next = (summed[3] - along_second[0], summed[4] - along_second[1])
            beta_step = times_complex(
                divide_complex(rho_next, rho_now), divide_complex(alpha_step, omega_step)
            )
            direction = residual + scale_complex(
                beta_step, direction - scale_complex(omega_step, image)
            )
            rho_now = rho_next
    return (evolved, residual)


UNROLL = 16
LEAD = 8
HALO = 4
POWERS = 2 * ITERS
ROUNDS = ITERS + 1
NEAR = -0.5 / SPACING**2 * COEFF_NEAR * HALF_STEP
FAR = -0.5 / SPACING**2 * COEFF_FAR * HALF_STEP
SIDES = ((0, -1), (0, 1), (-1, -1), (-1, 1), (1, -1), (1, 1), (-1, 0), (1, 0))


def sweep(count, plane, carry):
    width = UNROLL if count % UNROLL == 0 else 1

    def group(i, carry):
        for k in range(width):
            carry = plane(i * width + k, carry)
        return carry

    return lax.fori_loop(0, count // width, group, carry)


def power(vector):
    zero = jnp.zeros_like(vector[0][0])
    padded = vector + [(zero, zero)]
    out = [padded[0]]
    for j in range(1, len(padded)):
        out.append((padded[j][0] + padded[j - 1][0], padded[j][1] + padded[j - 1][1]))
    return out


def add_scaled(base, scale, vector):
    out = []
    for j in range(max(len(base), len(vector))):
        if j >= len(vector):
            out.append(base[j])
            continue
        term = times_complex(scale, vector[j])
        out.append((base[j][0] + term[0], base[j][1] + term[1]) if j < len(base) else term)
    return out


def negated(value):
    return (-value[0], -value[1])


def recurrence(gram):
    def times_gram(i, vector):
        total = None
        for j, value in enumerate(vector):
            term = times_complex(gram(i, j), value)
            total = term if total is None else (total[0] + term[0], total[1] + term[1])
        return total

    def conj_dot(left, right):
        total = None
        for a, b in zip(left, right):
            term = (a[0] * b[0] + a[1] * b[1], a[0] * b[1] - a[1] * b[0])
            total = term if total is None else (total[0] + term[0], total[1] + term[1])
        return total

    one = jnp.ones_like(gram(0, 0)[0])
    unit = [(one, jnp.zeros_like(one))]
    residual, direction, change = unit, unit, []
    rho = times_gram(0, residual)
    for iteration in range(ITERS):
        image = power(direction)
        alpha = divide_complex(rho, times_gram(0, image))
        half = add_scaled(residual, negated(alpha), image)
        second = power(half)
        applied = [times_gram(i, second) for i in range(len(second))]
        cross = conj_dot(half, applied)
        norm = conj_dot(second, applied)[0]
        omega = (cross[0] / norm, -cross[1] / norm)
        change = add_scaled(add_scaled(change, alpha, direction), omega, half)
        residual = add_scaled(half, negated(omega), second)
        if iteration + 1 < ITERS:
            rho_next = times_gram(0, residual)
            beta = times_complex(divide_complex(rho_next, rho), divide_complex(alpha, omega))
            inner = add_scaled(direction, negated(omega), image)
            direction = add_scaled(residual, beta, inner)
            rho = rho_next
    return change, residual


def solve_kernel(
    sizes,
    orb_hbm,
    pot_hbm,
    evolved_ref,
    residual_ref,
    fields,
    inner,
    basis,
    pot,
    diag,
    quot,
    quot_d,
    partial,
    gram_own,
    gram_all,
    send_sem,
    recv_sem,
    send_pot,
    recv_pot,
    send_gram,
    recv_gram,
    local_sem,
):
    size_x, size_y = sizes
    count, bx, by, nz = evolved_ref.shape[1:]
    gx, gy = (lax.axis_index("gx"), lax.axis_index("gyz"))
    me = gx * size_y + gy
    devices = size_x * size_y
    rows = slice(LEAD, LEAD + by)
    planes = slice(HALO, HALO + bx)

    def has(dx, dy):
        x, y = (gx + dx, gy + dy)
        inside = jnp.logical_and(x >= 0, x < size_x)
        return jnp.logical_and(inside, jnp.logical_and(y >= 0, y < size_y))

    def loads(o):
        return pltpu.make_async_copy(
            orb_hbm.at[:, o], fields.at[0, :, o, planes, rows, :], local_sem.at[o]
        )

    load_pot = pltpu.make_async_copy(
        pot_hbm, pot.at[pl.ds(2, bx), pl.ds(LEAD, by), :], local_sem.at[count]
    )
    load_pot.start()
    for o in range(count):
        loads(o).start()

    barrier = pltpu.get_barrier_semaphore()
    partners = 0
    for dx, dy in SIDES:
        there = has(dx, dy)
        partners = partners + there.astype(jnp.int32)

        @pl.when(there)
        def _():
            pl.semaphore_signal(
                barrier,
                inc=1,
                device_id={"gx": gx + dx, "gyz": gy + dy},
                device_id_type=pl.DeviceIdType.MESH,
            )

    def spans(d, first, extent, depth):
        if d == 0:
            return (pl.ds(first, extent), pl.ds(first, extent))
        if d > 0:
            return (pl.ds(first + extent - depth, depth), pl.ds(first - depth, depth))
        return (pl.ds(first, depth), pl.ds(first + extent, depth))

    def remote(src, dst, send, recv, dx, dy):
        return pltpu.make_async_remote_copy(
            src_ref=src,
            dst_ref=dst,
            send_sem=send,
            recv_sem=recv,
            device_id={"gx": gx + dx, "gyz": gy + dy},
            device_id_type=pl.DeviceIdType.MESH,
        )

    def halo_copy(r, o, k):
        dx, dy = SIDES[k]
        depth = 2 if (r == ROUNDS - 1 or (dx and dy)) else HALO
        sx, tx = spans(dx, HALO, bx, depth)
        sy, ty = spans(dy, LEAD, by, depth)
        return remote(
            fields.at[r, :, o, sx, sy, :],
            fields.at[r, :, o, tx, ty, :],
            send_sem.at[r, o, k],
            recv_sem.at[r, o, k],
            dx,
            dy,
        )

    def pot_copy(k):
        dx, dy = SIDES[k]
        sx, tx = spans(dx, 2, bx, 2)
        sy, ty = spans(dy, LEAD, by, 2)
        return remote(
            pot.at[sx, sy, :], pot.at[tx, ty, :], send_pot.at[k], recv_pot.at[k], dx, dy
        )

    def straight(k):
        return SIDES[k][0] == 0 or SIDES[k][1] == 0

    def ways(r):
        return [k for k in range(len(SIDES)) if r < ROUNDS - 1 or straight(k)]

    def send_halo(r, o):
        for k in ways(r):
            @pl.when(has(*SIDES[k]))
            def _():
                halo_copy(r, o, k).start()

    def wait_halo(r, o):
        for k in ways(r):
            @pl.when(has(-SIDES[k][0], -SIDES[k][1]))
            def _():
                halo_copy(r, o, k).wait_recv()

    def clear_edges(ref, halo):
        width, height = ref.shape[-3:-1]
        lead = ref.shape[:-3]
        flat = [()]
        for extent in lead:
            flat = [index + (i,) for index in flat for i in range(extent)]
        low, high = (LEAD - HALO, LEAD + by)

        def side(edge, first, stop):
            @pl.when(edge)
            def _():
                def clear(x, carry):
                    for index in flat:
                        ref[index + (x,)] = jnp.zeros((height, nz), jnp.float32)
                    return carry

                lax.fori_loop(first, stop, clear, 0)

        def band(edge, start):
            @pl.when(edge)
            def _():
                def clear(x, carry):
                    for index in flat:
                        ref[index + (x, slice(start, start + HALO))] = jnp.zeros(
                            (HALO, nz), jnp.float32
                        )
                    return carry

                lax.fori_loop(0, width, clear, 0)

        side(gx == 0, 0, halo)
        side(gx == size_x - 1, width - halo, width)
        band(gy == 0, low)
        band(gy == size_y - 1, high)

    for r in range(ROUNDS):
        clear_edges(fields.at[r], HALO)
    clear_edges(pot, 2)

    pl.semaphore_wait(barrier, partners)
    load_pot.wait()
    for k in range(len(SIDES)):
        if straight(k):
            @pl.when(has(*SIDES[k]))
            def _():
                pot_copy(k).start()
    for o in range(count):
        loads(o).wait()
        send_halo(0, o)

    for k in range(len(SIDES)):
        if straight(k):
            @pl.when(has(-SIDES[k][0], -SIDES[k][1]))
            def _():
                pot_copy(k).wait_recv()

    starts = list(range(-2, by - 5, 8))
    if starts[-1] != by - 6:
        starts.append(by - 6)

    def prepare(x, carry):
        for start in starts:
            span = slice(LEAD + start, LEAD + start + 8)
            d = HALF_STEP * (-1.5 * COEFF_SELF / SPACING**2 + pot[x, span, :])
            q = NEAR / (1.0 + d * d)
            diag[x, span, :] = d
            quot[x, span, :] = q
            quot_d[x, span, :] = q * d
        return carry

    lax.fori_loop(0, bx + 4, prepare, 0)
    for ref in (quot, quot_d):
        clear_edges(ref, 2)

    lane = lax.broadcasted_iota(jnp.int32, (8, nz), 1)

    def offdiagonal(ref, x, y):
        def at(dx, dy):
            return ref[x + dx, y + dy : y + dy + 8, :]

        center = at(0, 0)
        near = (at(1, 0) + at(-1, 0)) + (at(0, 1) + at(0, -1))
        far = (at(2, 0) + at(-2, 0)) + (at(0, 2) + at(0, -2))
        near = near + (
            jnp.where(lane < 1, 0.0, pltpu.roll(center, 1, 1))
            + jnp.where(lane >= nz - 1, 0.0, pltpu.roll(center, nz - 1, 1))
        )
        far = far + (
            jnp.where(lane < 2, 0.0, pltpu.roll(center, 2, 1))
            + jnp.where(lane >= nz - 2, 0.0, pltpu.roll(center, nz - 2, 1))
        )
        return near + (FAR / NEAR) * far, center

    def started(r, o, x, y):
        off_re, re = offdiagonal(fields.at[r, 0, o], x + HALO, LEAD + y)
        off_im, im = offdiagonal(fields.at[r, 1, o], x + HALO, LEAD + y)
        d = diag[x + 2, LEAD + y : LEAD + y + 8, :]
        return 2.0 * (NEAR * off_im + d * im), -2.0 * (NEAR * off_re + d * re)

    def outer(r, o, x, y):
        off_re, _ = offdiagonal(fields.at[r, 0, o], x + HALO, LEAD + y)
        off_im, _ = offdiagonal(fields.at[r, 1, o], x + HALO, LEAD + y)
        return -off_im, off_re

    def hats(x, y, re, im):
        span = slice(LEAD + y, LEAD + y + 8)
        q, qd = (quot[x + 2, span, :], quot_d[x + 2, span, :])
        return q * re + qd * im, q * im - qd * re

    def first_stage(r, o):
        apply = started if r == 0 else outer

        def plane(x, carry):
            for y in starts:
                span = slice(LEAD + y, LEAD + y + 8)
                re, im = apply(r, o, x, y)
                basis[2 * r, 0, o, x, span, :] = re
                basis[2 * r, 1, o, x, span, :] = im
                hat_re, hat_im = hats(x, y, re, im)
                inner[0, x + 2, span, :] = hat_re
                inner[1, x + 2, span, :] = hat_im
            return carry

        for x in (-2, -1, bx, bx + 1):
            for y in range(0, by, 8):
                span = slice(LEAD + y, LEAD + y + 8)
                re, im = apply(r, o, x, y)
                hat_re, hat_im = hats(x, y, re, im)
                inner[0, x + 2, span, :] = hat_re
                inner[1, x + 2, span, :] = hat_im
        sweep(bx, plane, 0)

    def second_stage(r, o):
        def plane(x, carry):
            for y in range(0, by, 8):
                span = slice(LEAD + y, LEAD + y + 8)
                off_re, _ = offdiagonal(inner.at[0], x + 2, LEAD + y)
                off_im, _ = offdiagonal(inner.at[1], x + 2, LEAD + y)
                re, im = -off_im, off_re
                basis[2 * r + 1, 0, o, x, span, :] = re
                basis[2 * r + 1, 1, o, x, span, :] = im
                hat_re, hat_im = hats(x, y, re, im)
                fields[r + 1, 0, o, x + HALO, span, :] = hat_re
                fields[r + 1, 1, o, x + HALO, span, :] = hat_im
            return carry

        sweep(bx, plane, 0)

    def last_stage(r, o):
        def plane(x, carry):
            for y in range(0, by, 8):
                span = slice(LEAD + y, LEAD + y + 8)
                re, im = outer(r, o, x, y)
                basis[2 * r, 0, o, x, span, :] = re
                basis[2 * r, 1, o, x, span, :] = im
            return carry

        sweep(bx, plane, 0)

    size = POWERS + 1
    zero = jnp.zeros((8, nz), jnp.float32)

    def products(j, o):
        def plane(x, sums):
            sums = list(sums)
            for y in range(0, by, 8):
                span = slice(LEAD + y, LEAD + y + 8)
                b_re, b_im = (basis[j, 0, o, x, span, :], basis[j, 1, o, x, span, :])
                for i in range(j):
                    a_re, a_im = (basis[i, 0, o, x, span, :], basis[i, 1, o, x, span, :])
                    sums[2 * i] = sums[2 * i] + (a_re * b_re + a_im * b_im)
                    sums[2 * i + 1] = sums[2 * i + 1] + (a_re * b_im - a_im * b_re)
                sums[2 * j] = sums[2 * j] + (b_re * b_re + b_im * b_im)
            return tuple(sums)

        sums = sweep(bx, plane, (zero,) * (2 * j + 1))
        packed = partial[o]
        for i in range(j + 1):
            packed = jnp.where(
                lane == i * size + j, jnp.sum(sums[2 * i], axis=1, keepdims=True), packed
            )
            if i < j:
                packed = jnp.where(
                    lane == j * size + i, jnp.sum(sums[2 * i + 1], axis=1, keepdims=True), packed
                )
        partial[o] = packed

    for o in range(count):
        partial[o] = zero
    for r in range(ROUNDS):
        last = r == ROUNDS - 1

        def advance(o, carry):
            wait_halo(r, o)
            if last:
                last_stage(r, o)
                products(2 * r, o)
            else:
                first_stage(r, o)
                second_stage(r, o)
                send_halo(r + 1, o)
            return carry

        lax.fori_loop(0, count, advance, 0)
        if not last:
            def gather(o, carry):
                products(2 * r, o)
                products(2 * r + 1, o)
                return carry

            lax.fori_loop(0, count, gather, 0)

    row = lax.broadcasted_iota(jnp.int32, (8, nz), 0)
    packed = zero
    for o in range(count):
        packed = jnp.where(row == o, jnp.sum(partial[o], axis=0, keepdims=True), packed)
    gram_own[...] = packed

    def gram_copy(dev, x, y):
        return pltpu.make_async_remote_copy(
            src_ref=gram_own,
            dst_ref=gram_all.at[dev],
            send_sem=send_gram.at[x * size_y + y],
            recv_sem=recv_gram.at[dev],
            device_id={"gx": x, "gyz": y},
            device_id_type=pl.DeviceIdType.MESH,
        )

    for dev in range(devices):
        @pl.when(me != dev)
        def _():
            gram_copy(me, dev // size_y, dev % size_y).start()

    gram_all[pl.ds(me, 1)] = packed[None]
    for dev in range(devices):
        @pl.when(me != dev)
        def _():
            gram_copy(dev, gx, gy).wait_recv()

    summed = gram_all[0]
    for dev in range(1, devices):
        summed = summed + gram_all[dev]

    def spread(index):
        return jnp.broadcast_to(summed[:, index : index + 1], (8, nz))

    values = {}

    def gram(i, j):
        if i > j:
            re, im = gram(j, i)
            return re, -im
        if (i, j) not in values:
            re = spread(i * size + j)
            values[i, j] = (re, spread(j * size + i) if i < j else jnp.zeros_like(re))
        return values[i, j]

    change, left = recurrence(gram)
    change = [(a / NEAR, b / NEAR) for a, b in change]

    for o in range(count):
        def own(value):
            return jnp.broadcast_to(value[o : o + 1], (8, nz))

        moves = [(own(a), own(b)) for a, b in change]
        rests = [(own(a), own(b)) for a, b in left]

        def finish(x, carry):
            for y in range(0, by, 8):
                span = slice(LEAD + y, LEAD + y + 8)
                s_re = s_im = r_re = r_im = None
                for j in range(size):
                    w_re, w_im = (basis[j, 0, o, x, span, :], basis[j, 1, o, x, span, :])
                    c = rests[j]
                    t_re = c[0] * w_re - c[1] * w_im
                    t_im = c[0] * w_im + c[1] * w_re
                    r_re = t_re if r_re is None else r_re + t_re
                    r_im = t_im if r_im is None else r_im + t_im
                    if j < len(moves):
                        c = moves[j]
                        t_re = c[0] * w_re - c[1] * w_im
                        t_im = c[0] * w_im + c[1] * w_re
                        s_re = t_re if s_re is None else s_re + t_re
                        s_im = t_im if s_im is None else s_im + t_im
                hat_re, hat_im = hats(x, y, s_re, s_im)
                out = slice(y, y + 8)
                evolved_ref[0, o, x, out, :] = fields[0, 0, o, x + HALO, span, :] + hat_re
                evolved_ref[1, o, x, out, :] = fields[0, 1, o, x + HALO, span, :] + hat_im
                residual_ref[0, o, x, out, :] = r_re
                residual_ref[1, o, x, out, :] = r_im
            return carry

        sweep(bx, finish, 0)

    for k in range(len(SIDES)):
        @pl.when(has(*SIDES[k]))
        def _():
            if straight(k):
                pot_copy(k).wait_send()
            for r in range(ROUNDS):
                if k in ways(r):
                    for o in range(count):
                        halo_copy(r, o, k).wait_send()

    for dev in range(devices):
        @pl.when(me != dev)
        def _():
            gram_copy(me, dev // size_y, dev % size_y).wait_send()


def powers(sizes, orbitals, potential):
    size_x, size_y = sizes
    _, count, bx, by, nz = orbitals.shape
    tall = by + 2 * LEAD
    devices = size_x * size_y
    dma = pltpu.SemaphoreType.DMA
    shape = jax.ShapeDtypeStruct(orbitals.shape, jnp.float32)

    def vmem(*dims):
        return pltpu.VMEM(dims, jnp.float32)

    return pl.pallas_call(
        functools.partial(solve_kernel, sizes),
        out_shape=(shape, shape),
        in_specs=[pl.BlockSpec(memory_space=pltpu.HBM)] * 2,
        out_specs=(pl.BlockSpec(memory_space=pltpu.VMEM),) * 2,
        scratch_shapes=[
            vmem(ROUNDS, 2, count, bx + 2 * HALO, tall, nz),
            vmem(2, bx + 4, tall, nz),
            vmem(POWERS + 1, 2, count, bx, tall, nz),
            vmem(bx + 4, tall, nz),
            vmem(bx + 4, tall, nz),
            vmem(bx + 4, tall, nz),
            vmem(bx + 4, tall, nz),
            vmem(count, 8, nz),
            vmem(8, nz),
            vmem(devices, 8, nz),
            dma((ROUNDS, count, len(SIDES))),
            dma((ROUNDS, count, len(SIDES))),
            dma((len(SIDES),)),
            dma((len(SIDES),)),
            dma((devices,)),
            dma((devices,)),
            dma((count + 1,)),
        ],
        compiler_params=pltpu.CompilerParams(
            collective_id=0, has_side_effects=True, vmem_limit_bytes=48 * 1024 * 1024
        ),
    )(orbitals, potential)


def step(sizes, orbitals, potential):
    _, count, bx, by, nz = orbitals.shape
    near = max(sizes) <= ROUNDS
    fits = (POWERS + 2 * ROUNDS) * count * (bx + 8) * (by + 16) * nz <= 1 << 23
    packs = count <= 8 and (POWERS + 1) ** 2 <= nz
    if near and fits and packs and by % 8 == 0 and nz == 128 and bx >= 4:
        return powers(sizes, orbitals, potential)
    return shards(orbitals, potential)


def solution(mesh):
    sizes = (mesh.shape["gx"], mesh.shape["gyz"])
    return jax.shard_map(
        functools.partial(step, sizes),
        mesh=mesh,
        in_specs=(P(None, "orb", "gx", "gyz", None), P("gx", "gyz", None)),
        out_specs=(P(None, "orb", "gx", "gyz", None), P(None, "orb", "gx", "gyz", None)),
        check_vma=False,
    )
```

time: 60.5 us -> 42.9 us (0.71)
  the two profiles are of different devices: /device:TPU:28 before, /device:TPU:0 now
where the time goes in v1:
time: 42.9 us; the launch traced here: 42.7 us
  Pallas kernels  38.7 us (90%)
  local copies, waits for them, and re-layouts  3.32 us (8%)
  between operations  0.65 us (2%)
    pallas_call x1, Pallas kernels, powers(): pl.pallas_call(functools.partial(solve_kernel, sizes), out_shape=(shape,...  38.7 us
    unnamed x6, local copies, waits for them, and re-layouts  3.32 us

profile of v1, /device:TPU:0, one launch (start us, length us, event | category | flops | bytes accessed | tf_op | source)
XLA Modules:
  0.0 42.7 jit_solution(4321847809771321617)
XLA Ops:
  0.6 0.0 copy-start
  0.6 1.0 %copy-done = f32[2,3,16,8,128]{4,3,2,1,0:T(8,128)S(1)} copy-done((f32[2,3,16,8,128]{4,3,2,1,0:T(8,128)S(1)}, f32[2,3,16,8,128]{4,3,2,1,0:T(8,128)}, u32[]{:S(2)}) %copy-start) | copy-done | bytes 393240
  1.6 0.0 copy-start.1
  1.6 0.8 %copy-done.1 = f32[16,8,128]{2,1,0:T(8,128)S(1)} copy-done((f32[16,8,128]{2,1,0:T(8,128)S(1)}, f32[16,8,128]{2,1,0:T(8,128)}, u32[]{:S(2)}) %copy-start.1) | copy-done | bytes 65560
  2.5 38.7 %shard_map.41 = (f32[2,3,16,8,128]{4,3,2,1,0:T(8,128)S(1)}, f32[2,3,16,8,128]{4,3,2,1,0:T(8,128)S(1)}) custom-call(f32[2,3,16,8,128]{4,3,2,1,0:T(8,128)S(1)} %copy-done, f32[16,8,128]{2,1,0:T(8,128)S(1)} %copy-done.1), custom_call_target="tpu_custom_call" | custom-call | tf_op jit(solution)/shard_map/pallas_call | solution.py:685
  41.2 0.7 %copy.6 = f32[2,3,16,8,128]{4,3,2,1,0:T(8,128)} copy(f32[2,3,16,8,128]{4,3,2,1,0:T(8,128)S(1)} %get-tuple-element.4) | data formatting | bytes 786432
  41.9 0.7 %copy.7 = f32[2,3,16,8,128]{4,3,2,1,0:T(8,128)} copy(f32[2,3,16,8,128]{4,3,2,1,0:T(8,128)S(1)} %get-tuple-element.5) | data formatting | bytes 786432
Async XLA Ops:
  0.6 1.0 %copy-start = (f32[2,3,16,8,128]{4,3,2,1,0:T(8,128)S(1)}, f32[2,3,16,8,128]{4,3,2,1,0:T(8,128)}, u32[]{:S(2)}) copy-start(f32[2,3,16,8,128]{4,3,2,1,0:T(8,128)} %orb_hbm.1) | copy-start | bytes 1179652
  1.6 0.8 %copy-start.1 = (f32[16,8,128]{2,1,0:T(8,128)S(1)}, f32[16,8,128]{2,1,0:T(8,128)}, u32[]{:S(2)}) copy-start(f32[16,8,128]{2,1,0:T(8,128)} %pot_hbm.1) | copy-start | bytes 196612

commit v2 on v1

--- a/solution.py
+++ b/solution.py
@@ -159,6 +159,7 @@
 UNROLL = 16
 LEAD = 8
 HALO = 4
+VMEM_LIMIT = 48000000
 POWERS = 2 * ITERS
 ROUNDS = ITERS + 1
 NEAR = -0.5 / SPACING**2 * COEFF_NEAR * HALF_STEP
@@ -166,8 +167,8 @@
 SIDES = ((0, -1), (0, 1), (-1, -1), (-1, 1), (1, -1), (1, 1), (-1, 0), (1, 0))
 
 
-def sweep(count, plane, carry):
-    width = UNROLL if count % UNROLL == 0 else 1
+def sweep(count, plane, carry, unroll=UNROLL):
+    width = unroll if count % unroll == 0 else 1
 
     def group(i, carry):
         for k in range(width):
@@ -201,19 +202,31 @@
     return (-value[0], -value[1])
 
 
+def plus(first, second):
+    if first is None:
+        return second
+    return (first[0] + second[0], first[1] + second[1])
+
+
+def conj_times(first, second):
+    return (
+        first[0] * second[0] + first[1] * second[1],
+        first[0] * second[1] - first[1] * second[0],
+    )
+
+
+def conj_dot(left, right):
+    total = None
+    for a, b in zip(left, right):
+        total = plus(total, conj_times(a, b))
+    return total
+
+
 def recurrence(gram):
     def times_gram(i, vector):
         total = None
         for j, value in enumerate(vector):
-            term = times_complex(gram(i, j), value)
-            total = term if total is None else (total[0] + term[0], total[1] + term[1])
-        return total
-
-    def conj_dot(left, right):
-        total = None
-        for a, b in zip(left, right):
-            term = (a[0] * b[0] + a[1] * b[1], a[0] * b[1] - a[1] * b[0])
-            total = term if total is None else (total[0] + term[0], total[1] + term[1])
+            total = plus(total, times_complex(gram(i, j), value))
         return total
 
     one = jnp.ones_like(gram(0, 0)[0])
@@ -225,19 +238,32 @@
         alpha = divide_complex(rho, times_gram(0, image))
         half = add_scaled(residual, negated(alpha), image)
         second = power(half)
+        change = add_scaled(change, alpha, direction)
+        if iteration + 1 == ITERS:
+            known = [times_gram(i, second[:-1]) for i in range(len(half))]
+            cross = conj_dot(half, known)
+            norm = conj_dot(second[:-1], known)[0]
+            return change, half, second, cross, norm
         applied = [times_gram(i, second) for i in range(len(second))]
         cross = conj_dot(half, applied)
         norm = conj_dot(second, applied)[0]
         omega = (cross[0] / norm, -cross[1] / norm)
-        change = add_scaled(add_scaled(change, alpha, direction), omega, half)
+        change = add_scaled(change, omega, half)
         residual = add_scaled(half, negated(omega), second)
-        if iteration + 1 < ITERS:
-            rho_next = times_gram(0, residual)
-            beta = times_complex(divide_complex(rho_next, rho), divide_complex(alpha, omega))
-            inner = add_scaled(direction, negated(omega), image)
-            direction = add_scaled(residual, beta, inner)
-            rho = rho_next
-    return change, residual
+        rho_next = times_gram(0, residual)
+        beta = times_complex(divide_complex(rho_next, rho), divide_complex(alpha, omega))
+        inner = add_scaled(direction, negated(omega), image)
+        direction = add_scaled(residual, beta, inner)
+        rho = rho_next
+
+
+def closing(column, half, second, cross, norm):
+    top = second[-1]
+    along = times_complex(top, conj_dot(half, column))
+    cross = plus(cross, along)
+    across = times_complex(top, conj_dot(second[:-1], column))
+    norm = norm + 2.0 * across[0] + (top[0] * top[0] + top[1] * top[1]) * column[-1][0]
+    return (cross[0] / norm, -cross[1] / norm)
 
 
 def solve_kernel(
@@ -253,6 +279,8 @@
     diag,
     quot,
     quot_d,
+    second_ref,
+    hat_ref,
     partial,
     gram_own,
     gram_all,
@@ -396,9 +424,8 @@
         band(gy == 0, low)
         band(gy == size_y - 1, high)
 
-    for r in range(ROUNDS):
-        clear_edges(fields.at[r], HALO)
     clear_edges(pot, 2)
+    clear_edges(fields.at[0], HALO)
 
     pl.semaphore_wait(barrier, partners)
     load_pot.wait()
@@ -409,13 +436,27 @@
                 pot_copy(k).start()
     for o in range(count):
         loads(o).wait()
-        send_halo(0, o)
+    late = lax.axis_index("orb") % 2 == 1
+
+    def send_first():
+        for o in range(count):
+            send_halo(0, o)
+
+    pl.when(jnp.logical_not(late))(send_first)
+
+    for r in range(1, ROUNDS):
+        clear_edges(fields.at[r], HALO)
+    for o in range(count):
+        for half in range(2):
+            partial[half, o] = jnp.zeros((8, nz), jnp.float32)
 
     for k in range(len(SIDES)):
         if straight(k):
             @pl.when(has(-SIDES[k][0], -SIDES[k][1]))
             def _():
                 pot_copy(k).wait_recv()
+
+    pl.when(late)(send_first)
 
     starts = list(range(-2, by - 5, 8))
     if starts[-1] != by - 6:
@@ -431,7 +472,7 @@
             quot_d[x, span, :] = q * d
         return carry
 
-    lax.fori_loop(0, bx + 4, prepare, 0)
+    sweep(bx + 4, prepare, 0, bx + 4)
     for ref in (quot, quot_d):
         clear_edges(ref, 2)
 
@@ -537,7 +578,8 @@
             return tuple(sums)
 
         sums = sweep(bx, plane, (zero,) * (2 * j + 1))
-        packed = partial[o]
+        half = 0 if j < POWERS else 1
+        packed = partial[half, o]
         for i in range(j + 1):
             packed = jnp.where(
                 lane == i * size + j, jnp.sum(sums[2 * i], axis=1, keepdims=True), packed
@@ -546,10 +588,58 @@
                 packed = jnp.where(
                     lane == j * size + i, jnp.sum(sums[2 * i + 1], axis=1, keepdims=True), packed
                 )
-        partial[o] = packed
-
-    for o in range(count):
-        partial[o] = zero
+        partial[half, o] = packed
+
+    row = lax.broadcasted_iota(jnp.int32, (8, nz), 0)
+
+    def gram_copy(half, dev, x, y):
+        return pltpu.make_async_remote_copy(
+            src_ref=gram_own.at[half],
+            dst_ref=gram_all.at[half, dev],
+            send_sem=send_gram.at[half, x * size_y + y],
+            recv_sem=recv_gram.at[half, dev],
+            device_id={"gx": x, "gyz": y},
+            device_id_type=pl.DeviceIdType.MESH,
+        )
+
+    def share(half):
+        packed = zero
+        for o in range(count):
+            packed = jnp.where(
+                row == o, jnp.sum(partial[half, o], axis=0, keepdims=True), packed
+            )
+        gram_own[half] = packed
+        gram_all[half, pl.ds(me, 1)] = packed[None]
+        for dev in range(devices):
+            @pl.when(me != dev)
+            def _():
+                gram_copy(half, me, dev // size_y, dev % size_y).start()
+
+    def shared(half):
+        for dev in range(devices):
+            @pl.when(me != dev)
+            def _():
+                gram_copy(half, dev, gx, gy).wait_recv()
+
+        summed = gram_all[half, 0]
+        for dev in range(1, devices):
+            summed = summed + gram_all[half, dev]
+        values = {}
+
+        def spread(index):
+            return jnp.broadcast_to(summed[:, index : index + 1], (8, nz))
+
+        def gram(i, j):
+            if i > j:
+                re, im = gram(j, i)
+                return re, -im
+            if (i, j) not in values:
+                re = spread(i * size + j)
+                values[i, j] = (re, spread(j * size + i) if i < j else jnp.zeros_like(re))
+            return values[i, j]
+
+        return gram
+
     for r in range(ROUNDS):
         last = r == ROUNDS - 1
 
@@ -565,95 +655,56 @@
             return carry
 
         lax.fori_loop(0, count, advance, 0)
-        if not last:
+        if last:
+            share(1)
+        else:
             def gather(o, carry):
                 products(2 * r, o)
                 products(2 * r + 1, o)
                 return carry
 
             lax.fori_loop(0, count, gather, 0)
-
-    row = lax.broadcasted_iota(jnp.int32, (8, nz), 0)
-    packed = zero
+            if r == ROUNDS - 2:
+                share(0)
+
+    change, halved, doubled, cross, norm = recurrence(shared(0))
+    change = [(a / NEAR, b / NEAR) for a, b in change]
+
+    def combine(o, x, span, coefs):
+        total = None
+        for j, c in enumerate(coefs):
+            term = times_complex(c, (basis[j, 0, o, x, span, :], basis[j, 1, o, x, span, :]))
+            total = plus(total, term)
+        return total
+
     for o in range(count):
-        packed = jnp.where(row == o, jnp.sum(partial[o], axis=0, keepdims=True), packed)
-    gram_own[...] = packed
-
-    def gram_copy(dev, x, y):
-        return pltpu.make_async_remote_copy(
-            src_ref=gram_own,
-            dst_ref=gram_all.at[dev],
-            send_sem=send_gram.at[x * size_y + y],
-            recv_sem=recv_gram.at[dev],
-            device_id={"gx": x, "gyz": y},
-            device_id_type=pl.DeviceIdType.MESH,
-        )
-
-    for dev in range(devices):
-        @pl.when(me != dev)
-        def _():
-            gram_copy(me, dev // size_y, dev % size_y).start()
-
-    gram_all[pl.ds(me, 1)] = packed[None]
-    for dev in range(devices):
-        @pl.when(me != dev)
-        def _():
-            gram_copy(dev, gx, gy).wait_recv()
-
-    summed = gram_all[0]
-    for dev in range(1, devices):
-        summed = summed + gram_all[dev]
-
-    def spread(index):
-        return jnp.broadcast_to(summed[:, index : index + 1], (8, nz))
-
-    values = {}
-
-    def gram(i, j):
-        if i > j:
-            re, im = gram(j, i)
-            return re, -im
-        if (i, j) not in values:
-            re = spread(i * size + j)
-            values[i, j] = (re, spread(j * size + i) if i < j else jnp.zeros_like(re))
-        return values[i, j]
-
-    change, left = recurrence(gram)
-    change = [(a / NEAR, b / NEAR) for a, b in change]
-
-    for o in range(count):
-        def own(value):
-            return jnp.broadcast_to(value[o : o + 1], (8, nz))
-
-        moves = [(own(a), own(b)) for a, b in change]
-        rests = [(own(a), own(b)) for a, b in left]
-
-        def finish(x, carry):
+        def own(values):
+            return [
+                tuple(jnp.broadcast_to(part[o : o + 1], (8, nz)) for part in value)
+                for value in values
+            ]
+
+        moves, halves, seconds = (own(change), own(halved), own(doubled))
+
+        def blend(x, carry):
             for y in range(0, by, 8):
                 span = slice(LEAD + y, LEAD + y + 8)
-                s_re = s_im = r_re = r_im = None
-                for j in range(size):
-                    w_re, w_im = (basis[j, 0, o, x, span, :], basis[j, 1, o, x, span, :])
-                    c = rests[j]
-                    t_re = c[0] * w_re - c[1] * w_im
-                    t_im = c[0] * w_im + c[1] * w_re
-                    r_re = t_re if r_re is None else r_re + t_re
-                    r_im = t_im if r_im is None else r_im + t_im
-                    if j < len(moves):
-                        c = moves[j]
-                        t_re = c[0] * w_re - c[1] * w_im
-                        t_im = c[0] * w_im + c[1] * w_re
-                        s_re = t_re if s_re is None else s_re + t_re
-                        s_im = t_im if s_im is None else s_im + t_im
-                hat_re, hat_im = hats(x, y, s_re, s_im)
                 out = slice(y, y + 8)
-                evolved_ref[0, o, x, out, :] = fields[0, 0, o, x + HALO, span, :] + hat_re
-                evolved_ref[1, o, x, out, :] = fields[0, 1, o, x + HALO, span, :] + hat_im
-                residual_ref[0, o, x, out, :] = r_re
-                residual_ref[1, o, x, out, :] = r_im
+                for ref, total in (
+                    (residual_ref, combine(o, x, span, halves)),
+                    (second_ref, combine(o, x, span, seconds)),
+                ):
+                    ref[0, o, x, out, :] = total[0]
+                    ref[1, o, x, out, :] = total[1]
+                hat = hats(x, y, residual_ref[0, o, x, out, :], residual_ref[1, o, x, out, :])
+                hat_ref[0, o, x, out, :] = hat[0]
+                hat_ref[1, o, x, out, :] = hat[1]
+                hat = hats(x, y, *combine(o, x, span, moves))
+                evolved_ref[0, o, x, out, :] = fields[0, 0, o, x + HALO, span, :] + hat[0]
+                evolved_ref[1, o, x, out, :] = fields[0, 1, o, x + HALO, span, :] + hat[1]
             return carry
 
-        sweep(bx, finish, 0)
+        sweep(bx, blend, 0)
 
     for k in range(len(SIDES)):
         @pl.when(has(*SIDES[k]))
@@ -665,10 +716,59 @@
                     for o in range(count):
                         halo_copy(r, o, k).wait_send()
 
-    for dev in range(devices):
-        @pl.when(me != dev)
-        def _():
-            gram_copy(me, dev // size_y, dev % size_y).wait_send()
+    gram = shared(1)
+    column = [gram(i, POWERS) for i in range(size)]
+    omega = closing(column, halved, doubled, cross, norm)
+    scaled = (omega[0] / NEAR, omega[1] / NEAR)
+
+    for o in range(count):
+        step_r, step_e = (
+            tuple(jnp.broadcast_to(part[o : o + 1], (8, nz)) for part in value)
+            for value in (omega, scaled)
+        )
+
+        def finish(x, carry):
+            for y in range(0, by, 8):
+                out = slice(y, y + 8)
+                for ref, other, coef, sign in (
+                    (residual_ref, second_ref, step_r, -1.0),
+                    (evolved_ref, hat_ref, step_e, 1.0),
+                ):
+                    term = times_complex(coef, (other[0, o, x, out, :], other[1, o, x, out, :]))
+                    ref[0, o, x, out, :] = ref[0, o, x, out, :] + sign * term[0]
+                    ref[1, o, x, out, :] = ref[1, o, x, out, :] + sign * term[1]
+            return carry
+
+        sweep(bx, finish, 0)
+
+    for half in range(2):
+        for dev in range(devices):
+            @pl.when(me != dev)
+            def _():
+                gram_copy(half, me, dev // size_y, dev % size_y).wait_send()
+
+
+def store_kernel(count, *refs):
+    sources, targets, sems = (refs[:count], refs[count : 2 * count], refs[-1])
+    copies = [
+        pltpu.make_async_copy(sources[k], targets[k], sems.at[k]) for k in range(count)
+    ]
+    for copy in copies:
+        copy.start()
+    for copy in copies:
+        copy.wait()
+
+
+def store(arrays):
+    count = len(arrays)
+    return pl.pallas_call(
+        functools.partial(store_kernel, count),
+        out_shape=tuple(jax.ShapeDtypeStruct(a.shape, a.dtype) for a in arrays),
+        in_specs=[pl.BlockSpec(memory_space=pltpu.VMEM)] * count,
+        out_specs=(pl.BlockSpec(memory_space=pltpu.HBM),) * count,
+        scratch_shapes=[pltpu.SemaphoreType.DMA((count,))],
+        compiler_params=pltpu.CompilerParams(vmem_limit_bytes=1 << 20),
+    )(*arrays)
 
 
 def powers(sizes, orbitals, potential):
@@ -682,7 +782,10 @@
     def vmem(*dims):
         return pltpu.VMEM(dims, jnp.float32)
 
-    return pl.pallas_call(
+    orbitals, potential = (
+        pltpu.with_memory_space_constraint(a, pltpu.HBM) for a in (orbitals, potential)
+    )
+    results = pl.pallas_call(
         functools.partial(solve_kernel, sizes),
         out_shape=(shape, shape),
         in_specs=[pl.BlockSpec(memory_space=pltpu.HBM)] * 2,
@@ -695,21 +798,24 @@
             vmem(bx + 4, tall, nz),
             vmem(bx + 4, tall, nz),
             vmem(bx + 4, tall, nz),
-            vmem(count, 8, nz),
-            vmem(8, nz),
-            vmem(devices, 8, nz),
+            vmem(*orbitals.shape),
+            vmem(*orbitals.shape),
+            vmem(2, count, 8, nz),
+            vmem(2, 8, nz),
+            vmem(2, devices, 8, nz),
             dma((ROUNDS, count, len(SIDES))),
             dma((ROUNDS, count, len(SIDES))),
             dma((len(SIDES),)),
             dma((len(SIDES),)),
-            dma((devices,)),
-            dma((devices,)),
+            dma((2, devices)),
+            dma((2, devices)),
             dma((count + 1,)),
         ],
         compiler_params=pltpu.CompilerParams(
-            collective_id=0, has_side_effects=True, vmem_limit_bytes=48 * 1024 * 1024
+            collective_id=0, has_side_effects=True, vmem_limit_bytes=VMEM_LIMIT
         ),
     )(orbitals, potential)
+    return store(results)
 
 
 def step(sizes, orbitals, potential):

time: 42.9 us -> 38.9 us (0.907)
  local copies, waits for them, and re-layouts: 3.32 us -> 0 us
  Pallas kernels: 38.7 us -> 38.2 us
    unnamed x6 -> x0, local copies, waits for them, and re-layouts: 3.32 us -> none
    pallas_call x1, Pallas kernels: 38.7 us -> 37.3 us  [powers(): pl.pallas_call(functools.partial(solve_kernel, sizes), out_shape=(shape,...]
    pallas_call x0 -> x1, Pallas kernels: none -> 0.89 us  [store(): pl.pallas_call(functools.partial(store_kernel, count), out_shape=tuple((j...]
where the time goes in v2:
time: 38.9 us; the launch traced here: 38.8 us
  Pallas kernels  38.2 us (98%)
  between operations  0.64 us (2%)
    pallas_call x1, Pallas kernels, powers(): pl.pallas_call(functools.partial(solve_kernel, sizes), out_shape=(shape,...  37.3 us
    pallas_call x1, Pallas kernels, store(): pl.pallas_call(functools.partial(store_kernel, count), out_shape=tuple((j...  0.89 us

profile of v2, /device:TPU:0, one launch (start us, length us, event | category | flops | bytes accessed | tf_op | source)
XLA Modules:
  0.0 38.8 jit_solution(18440784665767683113)
XLA Ops:
  0.6 37.3 %shard_map.41 = (f32[2,3,16,8,128]{4,3,2,1,0:T(8,128)S(1)}, f32[2,3,16,8,128]{4,3,2,1,0:T(8,128)S(1)}) custom-call(f32[2,3,16,8,128]{4,3,2,1,0:T(8,128)} %orb_hbm.1, f32[16,8,128]{2,1,0:T(8,128)} %pot_hbm.1), custom_call_target="tpu_custom_call" | custom-call | tf_op jit(solution)/shard_map/pallas_call | solution.py:788
  37.9 0.9 %shard_map.42 = (f32[2,3,16,8,128]{4,3,2,1,0:T(8,128)}, f32[2,3,16,8,128]{4,3,2,1,0:T(8,128)}) custom-call(f32[2,3,16,8,128]{4,3,2,1,0:T(8,128)S(1)} %get-tuple-element.4.refs_0_, f32[2,3,16,8,128]{4,3,2,1,0:T(8,128)S(1)} %get-tuple-element.5.refs_1_), custom_call_target="tpu_custom_call" | custom-call | tf_op jit(solution)/shard_map/pallas_call | solution.py:764

commit v3 on v2

--- a/solution.py
+++ b/solution.py
@@ -160,6 +160,7 @@
 LEAD = 8
 HALO = 4
 VMEM_LIMIT = 48000000
+LATER_NS = 1000
 POWERS = 2 * ITERS
 ROUNDS = ITERS + 1
 NEAR = -0.5 / SPACING**2 * COEFF_NEAR * HALF_STEP
@@ -456,7 +457,11 @@
             def _():
                 pot_copy(k).wait_recv()
 
-    pl.when(late)(send_first)
+    def hold_then_send():
+        pl.delay(LATER_NS)
+        send_first()
+
+    pl.when(late)(hold_then_send)
 
     starts = list(range(-2, by - 5, 8))
     if starts[-1] != by - 6:
@@ -594,8 +599,8 @@
 
     def gram_copy(half, dev, x, y):
         return pltpu.make_async_remote_copy(
-            src_ref=gram_own.at[half],
-            dst_ref=gram_all.at[half, dev],
+            src_ref=gram_own.at[half, 0:count],
+            dst_ref=gram_all.at[half, dev, 0:count],
             send_sem=send_gram.at[half, x * size_y + y],
             recv_sem=recv_gram.at[half, dev],
             device_id={"gx": x, "gyz": y},
@@ -624,6 +629,7 @@
         summed = gram_all[half, 0]
         for dev in range(1, devices):
             summed = summed + gram_all[half, dev]
+        summed = jnp.where(row < count, summed, 1.0)
         values = {}
 
         def spread(index):

time: 38.9 us -> 38.5 us (0.990)
  Pallas kernels: 38.2 us -> 37.7 us
    pallas_call x1, Pallas kernels: 37.3 us -> 36.8 us  [powers(): pl.pallas_call(functools.partial(solve_kernel, sizes), out_shape=(shape,...]
where the time goes in v3:
time: 38.5 us; the launch traced here: 38.3 us
  Pallas kernels  37.7 us (98%)
  between operations  0.64 us (2%)
    pallas_call x1, Pallas kernels, powers(): pl.pallas_call(functools.partial(solve_kernel, sizes), out_shape=(shape,...  36.8 us
    pallas_call x1, Pallas kernels, store(): pl.pallas_call(functools.partial(store_kernel, count), out_shape=tuple((j...  0.89 us

profile of v3, /device:TPU:0, one launch (start us, length us, event | category | flops | bytes accessed | tf_op | source)
XLA Modules:
  0.0 38.3 jit_solution(9515585043713639049)
XLA Ops:
  0.6 36.8 %shard_map.41 = (f32[2,3,16,8,128]{4,3,2,1,0:T(8,128)S(1)}, f32[2,3,16,8,128]{4,3,2,1,0:T(8,128)S(1)}) custom-call(f32[2,3,16,8,128]{4,3,2,1,0:T(8,128)} %orb_hbm.1, f32[16,8,128]{2,1,0:T(8,128)} %pot_hbm.1), custom_call_target="tpu_custom_call" | custom-call | tf_op jit(solution)/shard_map/pallas_call | solution.py:794
  37.4 0.9 %shard_map.42 = (f32[2,3,16,8,128]{4,3,2,1,0:T(8,128)}, f32[2,3,16,8,128]{4,3,2,1,0:T(8,128)}) custom-call(f32[2,3,16,8,128]{4,3,2,1,0:T(8,128)S(1)} %get-tuple-element.4.refs_0_, f32[2,3,16,8,128]{4,3,2,1,0:T(8,128)S(1)} %get-tuple-element.5.refs_1_), custom_call_target="tpu_custom_call" | custom-call | tf_op jit(solution)/shard_map/pallas_call | solution.py:770

commit v4 on v3

--- a/solution.py
+++ b/solution.py
@@ -435,12 +435,11 @@
             @pl.when(has(*SIDES[k]))
             def _():
                 pot_copy(k).start()
-    for o in range(count):
-        loads(o).wait()
     late = lax.axis_index("orb") % 2 == 1
 
     def send_first():
         for o in range(count):
+            loads(o).wait()
             send_halo(0, o)
 
     pl.when(jnp.logical_not(late))(send_first)
@@ -607,6 +606,14 @@
             device_id_type=pl.DeviceIdType.MESH,
         )
 
+    far_first = [
+        (dx, dy)
+        for dx in range(1 - size_x, size_x)
+        for dy in range(1 - size_y, size_y)
+        if dx or dy
+    ]
+    far_first.sort(key=lambda d: -abs(d[0]) - abs(d[1]))
+
     def share(half):
         packed = zero
         for o in range(count):
@@ -615,10 +622,10 @@
             )
         gram_own[half] = packed
         gram_all[half, pl.ds(me, 1)] = packed[None]
-        for dev in range(devices):
-            @pl.when(me != dev)
+        for dx, dy in far_first:
+            @pl.when(has(dx, dy))
             def _():
-                gram_copy(half, me, dev // size_y, dev % size_y).start()
+                gram_copy(half, me, gx + dx, gy + dy).start()
 
     def shared(half):
         for dev in range(devices):

time: 38.5 us -> 38.5 us (level)
  no operation moved by 1% of the time
where the time goes in v4:
time: 38.5 us; the launch traced here: 38.3 us
  Pallas kernels  37.7 us (98%)
  between operations  0.64 us (2%)
    pallas_call x1, Pallas kernels, powers(): pl.pallas_call(functools.partial(solve_kernel, sizes), out_shape=(shape,...  36.8 us
    pallas_call x1, Pallas kernels, store(): pl.pallas_call(functools.partial(store_kernel, count), out_shape=tuple((j...  0.89 us

profile of v4, /device:TPU:0, one launch (start us, length us, event | category | flops | bytes accessed | tf_op | source)
XLA Modules:
  0.0 38.3 jit_solution(827438351838738334)
XLA Ops:
  0.6 36.8 %shard_map.41 = (f32[2,3,16,8,128]{4,3,2,1,0:T(8,128)S(1)}, f32[2,3,16,8,128]{4,3,2,1,0:T(8,128)S(1)}) custom-call(f32[2,3,16,8,128]{4,3,2,1,0:T(8,128)} %orb_hbm.1, f32[16,8,128]{2,1,0:T(8,128)} %pot_hbm.1), custom_call_target="tpu_custom_call" | custom-call | tf_op jit(solution)/shard_map/pallas_call | solution.py:801
  37.4 0.9 %shard_map.42 = (f32[2,3,16,8,128]{4,3,2,1,0:T(8,128)}, f32[2,3,16,8,128]{4,3,2,1,0:T(8,128)}) custom-call(f32[2,3,16,8,128]{4,3,2,1,0:T(8,128)S(1)} %get-tuple-element.4.refs_0_, f32[2,3,16,8,128]{4,3,2,1,0:T(8,128)S(1)} %get-tuple-element.5.refs_1_), custom_call_target="tpu_custom_call" | custom-call | tf_op jit(solution)/shard_map/pallas_call | solution.py:777
